TPU v7x, 32 devices: a whole 2x2x4 slice. The times are simulated.
32 devices in a mesh: seq: 2 (over core), vocab: 16 (over z, y, x).
Axes of the slice: x: 2, y: 2, z: 4, core: 2. Of those that a mesh axis runs over, the one named last changes fastest.
Arguments:
- hidden: bfloat16 [1024, 8192], P('seq', 'vocab'), may hold values from -80 to 80
- weight: bfloat16 [8192, 8192], P('seq', 'vocab'), may hold values from -0.06629126 to 0.06629126, as said below
- tangent: bfloat16 [8192, 8192], P('seq', 'vocab'), may hold values from -0.0625 to 0.0625
- targets: int32 [1024], P('seq'), may hold values from 0 to 8191
Outputs:
- ggn: bfloat16 [8192, 8192], P('seq', 'vocab')
- token_loss: float32 [1024], P('seq')
Inputs may be any that keep to these rules, and one draw needn't show every extreme that they name: `weight`: entries of standard deviation about 8192 ** -0.5.
All inputs are finite; a program needn't handle non-finite values.
Results may differ from a plain program's by a relative error of at most 0.0065.
Values may be sent and summed in bfloat16 or wider, within the bound.
A program may use at most 64 MiB of HBM per device.

v0:
```python
import functools

import jax
import jax.numpy as jnp
from jax import lax
from jax.experimental import pallas as pl
from jax.experimental.pallas import tpu as pltpu
from jax.sharding import PartitionSpec as P

MESH = pl.DeviceIdType.MESH
PLANE, DEPTH = 4, 4
CHUNKS = 8
LEAD = 3
SKEW = 2


def gather_kernel(
    n, hidden, weight, tangent, target, flipped_out, term_out, loss_out,
    hid, flipped, wv, tv, acc, far, stats, term,
    recv, sent, pair_sent, load_sem, far_sent, far_recv, stat_sent, stat_recv, term_sem, out_sem,
):
    s = lax.axis_index("seq")
    v = lax.axis_index("vocab")
    half_n = n // 2
    tokens_own = hidden.shape[0]
    rows = hid.shape[1] // CHUNKS
    own_chunks = CHUNKS // 2
    width = wv.shape[2]
    z, y, x = v // PLANE, (v // 2) % 2, v % 2
    zz = z + s * (DEPTH - 1 - 2 * z)
    up_step = PLANE * (1 - 2 * s)
    base = half_n * s
    x_dev = (s, v + 1 - 2 * x)
    y_dev = (s, v + 2 - 4 * y)
    up_dev = (s, v + up_step)
    down_dev = (s, v - up_step)
    pair_dev = (1 - s, v)
    is_source = zz < DEPTH // 2

    load_w = pltpu.make_async_copy(weight, wv, load_sem.at[0])
    load_t = pltpu.make_async_copy(tangent, tv, load_sem.at[1])

    def own_load(i):
        c = own_chunks * s + i
        return pltpu.make_async_copy(
            hidden.at[pl.ds(i * rows, rows)],
            hid.at[v - base, pl.ds(pl.multiple_of(c * rows, rows), rows)],
            recv.at[v - base, c],
        )

    def pair_send(i):
        c = own_chunks * s + i
        k = v - half_n * (1 - s)
        return pltpu.make_async_remote_copy(
            src_ref=hidden.at[pl.ds(i * rows, rows)],
            dst_ref=hid.at[k, pl.ds(pl.multiple_of(c * rows, rows), rows)],
            send_sem=pair_sent.at[i],
            recv_sem=recv.at[k, c],
            device_id=pair_dev,
            device_id_type=MESH,
        )

    barrier = pltpu.get_barrier_semaphore()

    def greet(d, carry):
        pl.semaphore_signal(barrier, inc=1, device_id=(s, (v + d) % n), device_id_type=MESH)
        return carry

    pl.semaphore_signal(barrier, inc=1, device_id=pair_dev, device_id_type=MESH)
    lax.fori_loop(1, n, greet, 0)

    @pl.when(is_source)
    def _():
        for i in range(own_chunks):
            own_load(i).start()

    load_w.start()
    load_t.start()

    def clear(i, carry):
        acc[pl.ds(i * rows, rows), :] = jnp.zeros((rows, acc.shape[1]), jnp.float32)
        return carry

    lax.fori_loop(0, CHUNKS, clear, 0)
    pl.semaphore_wait(barrier, n)

    @pl.when(zz >= DEPTH // 2)
    def _():
        for i in range(own_chunks):
            pair_send(i).start()

    def place(cc):
        return (cc + own_chunks * s) % CHUNKS

    def copy(link, k, c, device):
        piece = hid.at[k, pl.ds(pl.multiple_of(c * rows, rows), rows)]
        return pltpu.make_async_remote_copy(
            src_ref=piece,
            dst_ref=piece,
            send_sem=sent.at[link, k, c],
            recv_sem=recv.at[k, c],
            device_id=device,
            device_id_type=MESH,
        )

    def routes(k, c, cc, dx, dy, szz):
        last = cc == 3
        odd = (cc + cc // 4) % 2 == 1
        even = jnp.logical_not(odd)
        column = dx + dy == 0
        inplane = jnp.logical_or(jnp.logical_not(last), szz == zz)
        along = jnp.logical_or(last, column)
        via_x = jnp.logical_and(jnp.logical_and(dx == 0, dy == 1), odd)
        via_y = jnp.logical_and(jnp.logical_and(dx == 1, dy == 0), even)
        go_up = jnp.logical_and(along, jnp.logical_and(zz >= szz, zz < DEPTH - 1))
        go_down = jnp.logical_and(along, jnp.logical_and(zz == 1, szz == 1))
        return (
            (go_up, copy(2, k, c, up_dev)),
            (go_down, copy(3, k, c, down_dev)),
            (jnp.logical_and(inplane, jnp.logical_or(column, via_x)), copy(0, k, c, x_dev)),
            (jnp.logical_and(inplane, jnp.logical_or(column, via_y)), copy(1, k, c, y_dev)),
        )

    def item(q, cc):
        r, i = q // 2, q % 2
        dx, dy = r % 2, r // 2
        first = jnp.where(zz >= 1, 1, 0)
        szz = first + i * (1 - 2 * first)
        src_z = szz + s * (DEPTH - 1 - 2 * szz)
        k = src_z * PLANE + ((y + dy) % 2) * 2 + (x + dx) % 2 - base
        return k, place(cc), dx, dy, szz

    def send_own(cc):
        @pl.when(jnp.logical_and(is_source, cc < CHUNKS))
        def _():
            k, c = v - base, place(cc)
            copy(0, k, c, x_dev).wait_recv()
            for condition, route in routes(k, c, cc, 0, 0, zz):
                @pl.when(condition)
                def _():
                    route.start()

    def lead(cc, carry):
        send_own(cc)
        return carry

    lax.fori_loop(0, LEAD, lead, 0)
    load_w.wait()
    load_t.wait()

    def far_copy(j):
        c = own_chunks * (1 - s) + j
        return pltpu.make_async_remote_copy(
            src_ref=acc.at[pl.ds(pl.multiple_of(c * rows, rows), rows)],
            dst_ref=far.at[pl.ds(pl.multiple_of(j * rows, rows), rows)],
            send_sem=far_sent.at[j],
            recv_sem=far_recv.at[j],
            device_id=pair_dev,
            device_id_type=MESH,
        )

    def step(t, carry):
        send_own(t + LEAD)

        def one(q, inner):
            r = q // 2
            cc = t - SKEW * (r % 2 + r // 2)

            @pl.when(jnp.logical_and(cc >= 0, cc < CHUNKS))
            def _():
                k, c, dx, dy, szz = item(q, cc)
                mine = jnp.logical_and(dx + dy == 0, szz == zz)

                @pl.when(jnp.logical_not(mine))
                def _():
                    copy(0, k, c, x_dev).wait_recv()
                    for condition, route in routes(k, c, cc, dx, dy, szz):
                        @pl.when(condition)
                        def _():
                            route.start()

                span = pl.ds(pl.multiple_of(c * rows, rows), rows)
                piece = hid[k, span, :]
                acc[span, :width] += jnp.dot(piece, wv[k], preferred_element_type=jnp.float32)
                acc[span, width:] += jnp.dot(piece, tv[k], preferred_element_type=jnp.float32)
                flipped[k, :, span] = piece.T

            return inner

        lax.fori_loop(0, 8, one, 0)

        @pl.when(jnp.logical_and(t >= own_chunks + 2 * SKEW, t < CHUNKS + 2 * SKEW))
        def _():
            far_copy(t - 2 * SKEW - own_chunks).start()

        return carry

    lax.fori_loop(0, CHUNKS + 2 * SKEW, step, 0)

    flip_copy = pltpu.make_async_copy(flipped, flipped_out, out_sem.at[0])
    flip_copy.start()

    own_base = tokens_own * s
    lanes = 128

    def local_stats(j, carry):
        far_copy(j).wait_recv()
        span = pl.ds(pl.multiple_of(own_base + j * rows, rows), rows)
        near = pl.ds(pl.multiple_of(j * rows, rows), rows)
        both = acc[span, :] + far[near, :]
        far[near, :] = both
        logits, slope = both[:, :width], both[:, width:]
        top = jnp.max(logits, axis=1, keepdims=True)
        e = jnp.exp(logits - top)
        total = jnp.sum(e, axis=1, keepdims=True)
        weighted = jnp.sum(e * slope, axis=1, keepdims=True)
        wanted = jnp.broadcast_to(target[:, near], (lanes, rows)).T[:, 0:1]
        columns = lax.broadcasted_iota(jnp.int32, logits.shape, 1) + v * width
        picked = jnp.sum(jnp.where(columns == wanted, logits, 0.0), axis=1, keepdims=True)
        lane = lax.broadcasted_iota(jnp.int32, (rows, lanes), 1)
        packed = jnp.where(lane == 0, top, jnp.where(lane == 1, total, jnp.where(lane == 2, weighted, picked)))
        stats[0, :, near] = packed.T[:4]
        return carry

    lax.fori_loop(0, own_chunks, local_stats, 0)

    def stat_copy(d):
        return pltpu.make_async_remote_copy(
            src_ref=stats.at[0],
            dst_ref=stats.at[d],
            send_sem=stat_sent.at[d],
            recv_sem=stat_recv.at[d],
            device_id=(s, (v + d) % n),
            device_id_type=MESH,
        )

    def stat_start(d, carry):
        stat_copy(d).start()
        return carry

    def stat_wait(d, carry):
        stat_copy(d).wait()
        return carry

    lax.fori_loop(1, n, stat_start, 0)

    def far_wait(j, carry):
        far_copy(j).wait_send()
        return carry

    lax.fori_loop(0, own_chunks, far_wait, 0)

    def drain(t, carry):
        k, c, dx, dy, szz = item(t % 8, t // 8)
        for condition, route in routes(k, c, t // 8, dx, dy, szz):
            @pl.when(condition)
            def _():
                route.wait_send()
        return carry

    lax.fori_loop(0, 8 * CHUNKS, drain, 0)

    @pl.when(zz >= DEPTH // 2)
    def _():
        for i in range(own_chunks):
            pair_send(i).wait_send()

    lax.fori_loop(1, n, stat_wait, 0)
    every = stats[...]
    tops = every[:, 0, :]
    row_top = jnp.max(tops, axis=0, keepdims=True)
    scale = jnp.exp(tops - row_top)
    totals = jnp.sum(scale * every[:, 1, :], axis=0, keepdims=True)
    tangent_sum = jnp.sum(scale * every[:, 2, :], axis=0, keepdims=True)
    picked = jnp.sum(every[:, 3, :], axis=0, keepdims=True)
    expect = tangent_sum / totals
    loss_out[...] = row_top + jnp.log(totals) - picked
    line = lax.broadcasted_iota(jnp.int32, (lanes, tokens_own), 0)
    spread = jnp.where(line == 0, row_top, jnp.where(line == 1, totals, expect))
    upright = spread.T

    for j in range(own_chunks):
        near = pl.ds(j * rows, rows)
        part = upright[j * rows : (j + 1) * rows]
        both = far[near, :]
        value = (
            jnp.exp(both[:, :width] - part[:, 0:1]) / part[:, 1:2] * (both[:, width:] - part[:, 2:3])
        )
        term[pl.ds(pl.multiple_of(own_base + j * rows, rows), rows), :] = value.astype(term.dtype)

    own_span = pl.ds(pl.multiple_of(own_base, tokens_own), tokens_own)
    swap = pltpu.make_async_remote_copy(
        src_ref=term.at[own_span],
        dst_ref=term.at[own_span],
        send_sem=term_sem.at[0],
        recv_sem=term_sem.at[1],
        device_id=pair_dev,
        device_id_type=MESH,
    )
    swap.start()
    swap.wait()
    term_copy = pltpu.make_async_copy(term, term_out, out_sem.at[1])
    term_copy.start()
    term_copy.wait()
    flip_copy.wait()


def product_kernel(flipped, term, out):
    depth = flipped.shape[1]
    for i in range(2):
        out[i * depth : (i + 1) * depth] = jnp.dot(flipped[i], term[...], preferred_element_type=jnp.float32).astype(out.dtype)


def relayed(n, hidden, weight, tangent, targets):
    half_n = n // 2
    tokens_own, shard = hidden.shape
    width = weight.shape[1]
    tokens = 2 * tokens_own
    rows = tokens // CHUNKS
    blocks = (half_n, shard, width)
    hbm = pl.BlockSpec(memory_space=pl.ANY)
    vmem = pl.BlockSpec(memory_space=pltpu.VMEM)
    dma = pltpu.SemaphoreType.DMA
    flipped, term, loss = pl.pallas_call(
        functools.partial(gather_kernel, n),
        name="gather_logits",
        out_shape=(
            jax.ShapeDtypeStruct((half_n, shard, tokens), hidden.dtype),
            jax.ShapeDtypeStruct((tokens, width), jnp.bfloat16),
            jax.ShapeDtypeStruct((1, tokens_own), jnp.float32),
        ),
        in_specs=[hbm, hbm, hbm, vmem],
        out_specs=(hbm, hbm, vmem),
        scratch_shapes=[
            pltpu.VMEM((half_n, tokens, shard), hidden.dtype),
            pltpu.VMEM((half_n, shard, tokens), hidden.dtype),
            pltpu.VMEM(blocks, weight.dtype),
            pltpu.VMEM(blocks, tangent.dtype),
            pltpu.VMEM((tokens, 2 * width), jnp.float32),
            pltpu.VMEM((tokens_own, 2 * width), jnp.float32),
            pltpu.VMEM((n, 4, tokens_own), jnp.float32),
            pltpu.VMEM((tokens, width), jnp.bfloat16),
            dma((half_n, CHUNKS)),
            dma((4, half_n, CHUNKS)),
            dma((CHUNKS // 2,)),
            dma((2,)),
            dma((CHUNKS // 2,)),
            dma((CHUNKS // 2,)),
            dma((n,)),
            dma((n,)),
            dma((2,)),
            dma((2,)),
        ],
        compiler_params=pltpu.CompilerParams(collective_id=0, has_side_effects=True),
    )(hidden, weight.reshape(blocks), tangent.reshape(blocks), targets.reshape(1, tokens_own))
    ggn = pl.pallas_call(
        product_kernel,
        name="product",
        grid=(half_n // 2,),
        out_shape=jax.ShapeDtypeStruct(weight.shape, jnp.bfloat16),
        in_specs=[
            pl.BlockSpec((2, shard, tokens), lambda k: (k, 0, 0)),
            pl.BlockSpec((tokens, width), lambda k: (0, 0)),
        ],
        out_specs=pl.BlockSpec((2 * shard, width), lambda k: (k, 0)),
    )(flipped, term)
    return ggn, loss.reshape(tokens_own)


def partner(value, axis, stride):
    mask = 2**stride
    pairs = [(source, source ^ mask) for source in range(lax.axis_size(axis))]
    return lax.ppermute(value, axis, pairs)


def on_device(hidden, weight, tangent, targets):
    n = lax.axis_size("vocab")
    if n == PLANE * DEPTH and lax.axis_size("seq") == 2 and hidden.shape[1] % 128 == 0:
        return relayed(n, hidden, weight, tangent, targets)
    vocab_index = lax.axis_index("vocab")
    shard_width = weight.shape[1]
    half_width = weight.shape[0]
    whole = lax.all_gather(hidden, "vocab", axis=1, tiled=True)
    seq_index = lax.axis_index("seq")
    own_part = lax.dynamic_slice_in_dim(whole, seq_index * half_width, half_width, 1)
    far_part = lax.dynamic_slice_in_dim(whole, (1 - seq_index) * half_width, half_width, 1)
    received = partner(far_part, "seq", 0)
    leading = jnp.where(seq_index == 0, own_part, received)
    trailing = jnp.where(seq_index == 0, received, own_part)
    stacked = jnp.concatenate([leading, trailing], axis=0)
    partial_logits = jnp.dot(stacked, weight, preferred_element_type=jnp.float32)
    partial_tangent = jnp.dot(stacked, tangent, preferred_element_type=jnp.float32)
    logits, tangent_logits = (
        lax.psum_scatter(partial_logits, "seq", scatter_dimension=0, tiled=True),
        lax.psum_scatter(partial_tangent, "seq", scatter_dimension=0, tiled=True),
    )
    local_target = targets - vocab_index * shard_width
    columns_ids = jnp.arange(shard_width, dtype=jnp.int32)
    picked_local = jnp.sum(
        jnp.where(columns_ids[None, :] == local_target[:, None], logits, jnp.float32(0.0)), axis=1
    )
    local_top = jnp.max(logits, axis=1)
    row_top = lax.pmax(local_top, "vocab")
    exp_logits = jnp.exp(logits - row_top[:, None])
    totals, tangent_sum, picked = lax.psum(
        (jnp.sum(exp_logits, axis=1), jnp.sum(exp_logits * tangent_logits, axis=1), picked_local),
        "vocab",
    )
    expect = tangent_sum / totals
    token_loss = row_top + jnp.log(totals) - picked
    weight_term = (exp_logits / totals[:, None] * (tangent_logits - expect[:, None])).astype(
        jnp.bfloat16
    )
    far_term = partner(weight_term, "seq", 0)
    lead_term = jnp.where(seq_index == 0, weight_term, far_term)
    trail_term = jnp.where(seq_index == 0, far_term, weight_term)
    all_terms = jnp.concatenate([lead_term, trail_term], axis=0)
    ggn = jnp.einsum("td,tv->dv", stacked, all_terms, preferred_element_type=jnp.float32).astype(
        jnp.bfloat16
    )
    return (ggn, token_loss)


def solution(mesh):
    in_specs = (P("seq", "vocab"), P("seq", "vocab"), P("seq", "vocab"), P("seq"))
    out_specs = (P("seq", "vocab"), P("seq"))
    return jax.shard_map(
        on_device, mesh=mesh, in_specs=in_specs, out_specs=out_specs, check_vma=False
    )
```

profile of v0, /device:TPU:0, one launch (start us, length us, event | category | flops | bytes accessed | tf_op | source)
XLA Modules:
  0.0 95.9 jit_solution(14656903061962893131)
XLA Ops:
  0.6 85.9 %gather_logits.1 = (bf16[8,512,1024]{2,1,0:T(8,128)(2,1)}, bf16[1024,512]{1,0:T(8,128)(2,1)}, f32[1,512]{1,0:T(1,128)}) custom-call(bf16[512,512]{1,0:T(8,128)(2,1)} %hidden.1, bf16[8,512,512]{2,1,0:T(8,128)(2,1)} %bitcast.4, bf16[8,512,512]{2,1,0:T(8,128)(2,1)} %bitcast.5, s32[1,512]{1,0:T(1,128)} %bitcast.6), custom_call_target="tpu_custom_call" | custom-call | tf_op jit(solution)/shard_map/gather_logits/pallas_call | solution.py:324
  86.6 0.0 copy-start
  86.6 8.7 %product.1 = bf16[4096,512]{1,0:T(8,128)(2,1)} custom-call(bf16[8,512,1024]{2,1,0:T(8,128)(2,1)} %get-tuple-element.5.flipped, bf16[1024,512]{1,0:T(8,128)(2,1)} %get-tuple-element.6.term), custom_call_target="tpu_custom_call" | custom-call | tf_op jit(solution)/shard_map/product/pallas_call | solution.py:356
  95.3 0.0 copy-done
  95.3 0.6 copy.7
Async XLA Ops:
  86.6 8.8 %copy-start = (f32[1,512]{1,0:T(1,128)S(1)}, f32[1,512]{1,0:T(1,128)}, u32[]{:S(2)}) copy-start(f32[1,512]{1,0:T(1,128)} %get-tuple-element.7) | copy-start | bytes 6148
where the time goes:
time: 96.1 us; the launch traced here: 95.9 us
  Pallas kernels  94.7 us (99%)
    pallas_call x1, Pallas kernels, relayed(): pl.pallas_call(functools.partial(gather_kernel, n), name='gather_logits',...  85.9 us
    pallas_call x1, Pallas kernels, relayed(): pl.pallas_call(product_kernel, name='product', grid=(half_n // 2,), out_s...  8.74 us

commit v1 on v0

v1 whole, which is shorter than its diff:
```python
import functools

import jax
import jax.numpy as jnp
from jax import lax
from jax.experimental import pallas as pl
from jax.experimental.pallas import tpu as pltpu
from jax.sharding import PartitionSpec as P

MESH = pl.DeviceIdType.MESH
PLANE, DEPTH = 4, 4
CHUNKS = 8
GROUPS = CHUNKS // 2
LEAD = 3
LAGS = ((0, 0, 2, 2, 2, 2, 4, 4), (0, 0, 2, 2, 2, 2, 4, 4), (0, 0, 2, 2, 2, 2, 4, 4), (0, 0, 2, 2, 2, 2, 4, 4))
ORDERS = ((0, 1, 2, 3, 4, 5, 6, 7), (0, 1, 2, 3, 4, 5, 6, 7), (0, 1, 2, 3, 4, 5, 6, 7), (0, 1, 2, 3, 4, 5, 6, 7))
TALL = (0, 0, 0, 255, 0, 0, 0, 0)
DEEP = (0, 0, 0, 15, 0, 0, 0, 0)
VIA = (0, 255, 0, 255, 255, 0, 255, 0)
LANES = 128


def links_used(zz, y, x):
    used = [0, 0, 0, 0]
    for c in range(CHUNKS):
        for item in range(8):
            szz, dy, dx = item // 4, item // 2 % 2, item % 2
            spot = (y + dy) % 2 * 2 + (x + dx) % 2
            tall = TALL[c] >> (szz * 4 + spot) & 1
            deep = DEEP[c] >> spot & 1 and szz == 1
            via = VIA[c] >> (szz * 4 + spot) & 1
            column = dx + dy == 0
            inplane = not (zz > szz and tall or zz < szz and deep)
            used[0] += inplane and (column or (dx == 0 and dy == 1 and via == 1))
            used[1] += inplane and (column or (dx == 1 and dy == 0 and via == 0))
            used[2] += (column or tall) and zz >= szz and zz < DEPTH - 1
            used[3] += (column or deep) and zz == 1 and szz == 1
    return [int(u) for u in used]


def packed(values, bits):
    word = sum(value << (bits * i) for i, value in enumerate(values))
    return word - (word >> 31 << 32)


def pick(index, values):
    chosen = jnp.int32(values[0])
    for i, value in enumerate(values[1:]):
        chosen = jnp.where(index == i + 1, jnp.int32(value), chosen)
    return chosen


def field(word, index, bits):
    return (word >> (index * bits)) & (2**bits - 1)


def gather_kernel(
    n, hidden, weight, tangent, targets, total, last, term, loss_out,
    hid, flipped, staged, wv, tv, part, far, stats, target, target_pair, wanted,
    recv, sent, pair_recv, pair_sent, load_sem, far_sent, far_recv,
    stat_sent, stat_recv, target_sem, hello,
):
    s = lax.axis_index("seq")
    v = lax.axis_index("vocab")
    half_n = n // 2
    rows = hid.shape[1]
    half = rows // 2
    group_rows = 2 * rows
    width = wv.shape[2]
    z, y, x = v // PLANE, (v // 2) % 2, v % 2
    zz = z + s * (DEPTH - 1 - 2 * z)
    up_step = PLANE * (1 - 2 * s)
    x_dev = (s, v + 1 - 2 * x)
    y_dev = (s, v + 2 - 4 * y)
    up_dev = (s, v + up_step)
    down_dev = (s, v - up_step)
    pair_dev = (1 - s, v)
    is_source = zz < DEPTH // 2
    has_up = zz < DEPTH - 1
    has_down = zz > 0
    along_count = has_up.astype(jnp.int32) + has_down.astype(jnp.int32)
    own_k = jnp.where(is_source, v - half_n * s, 0)
    pair_k = jnp.where(is_source, 0, v - half_n * (1 - s))
    lag_word = pick(zz, [packed(lags, 4) for lags in LAGS])
    order_word = pick(zz, [packed(order, 3) for order in ORDERS])
    last_lag = pick(zz, [max(lags) for lags in LAGS])
    finish_lag = jnp.where(is_source, 4, 2)

    mine = pl.ds(pl.multiple_of(s * half, half), half)
    theirs = pl.ds(pl.multiple_of((1 - s) * half, half), half)

    load_w = pltpu.make_async_copy(weight, wv, load_sem.at[0])
    load_t = pltpu.make_async_copy(tangent, tv, load_sem.at[1])
    load_target = pltpu.make_async_copy(targets, target, load_sem.at[2])

    own_load = pltpu.make_async_copy(hidden, hid.at[pl.ds(own_k * CHUNKS, CHUNKS), mine], load_sem.at[3])
    stage = pltpu.make_async_copy(hidden, staged, load_sem.at[3])

    def pair_copy(k, c, span):
        return pltpu.make_async_remote_copy(
            src_ref=staged.at[c],
            dst_ref=hid.at[k * CHUNKS + c, span],
            send_sem=pair_sent.at[0],
            recv_sem=pair_recv.at[c],
            device_id=pair_dev,
            device_id_type=MESH,
        )

    def bulk(ref, semaphore):
        return pltpu.make_async_remote_copy(
            src_ref=ref,
            dst_ref=ref,
            send_sem=semaphore,
            recv_sem=semaphore,
            device_id=pair_dev,
            device_id_type=MESH,
        )

    def greet(semaphore, device):
        pl.semaphore_signal(semaphore, inc=1, device_id=device, device_id_type=MESH)

    def greet_along(semaphore):
        @pl.when(has_up)
        def _():
            greet(semaphore, up_dev)

        @pl.when(has_down)
        def _():
            greet(semaphore, down_dev)

    barrier = pltpu.get_barrier_semaphore()
    greet(barrier, pair_dev)
    greet(barrier, x_dev)
    greet(barrier, y_dev)
    greet_along(barrier)

    @pl.when(is_source)
    def _():
        own_load.start()

    @pl.when(jnp.logical_not(is_source))
    def _():
        stage.start()

    load_target.start()
    load_w.start()
    load_t.start()

    def clear(i, carry):
        part[i] = jnp.zeros(part.shape[1:], jnp.float32)
        total[i] = jnp.zeros(total.shape[1:], jnp.float32)
        return carry

    lax.fori_loop(0, CHUNKS, clear, 0)
    loss_out[...] = jnp.zeros_like(loss_out)
    load_target.wait()
    pl.semaphore_wait(barrier, 3 + along_count)
    greet(hello.at[0], x_dev)
    pair_target = pltpu.make_async_remote_copy(
        src_ref=target,
        dst_ref=target_pair,
        send_sem=target_sem.at[0],
        recv_sem=target_sem.at[1],
        device_id=pair_dev,
        device_id_type=MESH,
    )
    pair_target.start()

    @pl.when(jnp.logical_not(is_source))
    def _():
        stage.wait()

        def give(c, carry):
            pair_copy(pair_k, c, mine).start()
            return carry

        lax.fori_loop(0, CHUNKS, give, 0)

    @pl.when(is_source)
    def _():
        own_load.wait()

    def copy(link, k, c, device, span):
        piece = hid.at[k * CHUNKS + c, span]
        return pltpu.make_async_remote_copy(
            src_ref=piece,
            dst_ref=piece,
            send_sem=sent.at[link],
            recv_sem=recv.at[k, c],
            device_id=device,
            device_id_type=MESH,
        )

    def routes(k, c, dx, dy, szz, span):
        column = dx + dy == 0
        spot = ((y + dy) % 2) * 2 + (x + dx) % 2
        word = pick(c, [TALL[i] | VIA[i] << 8 | DEEP[i] << 20 for i in range(CHUNKS)])
        place = szz * 4 + spot
        tall = field(word, place, 1) == 1
        via = field(word, place + 8, 1)
        deep = field(word, place + 16, 1) == 1
        along = jnp.logical_or(
            jnp.logical_and(zz > szz, tall), jnp.logical_and(zz < szz, deep)
        )
        inplane = jnp.logical_not(along)
        via_x = jnp.logical_and(jnp.logical_and(dx == 0, dy == 1), via == 1)
        via_y = jnp.logical_and(jnp.logical_and(dx == 1, dy == 0), via == 0)
        go_up = jnp.logical_and(jnp.logical_or(column, tall), jnp.logical_and(zz >= szz, has_up))
        go_down = jnp.logical_and(jnp.logical_or(column, deep), jnp.logical_and(zz == 1, szz == 1))
        return (
            (go_up, copy(2, k, c, up_dev, span)),
            (go_down, copy(3, k, c, down_dev, span)),
            (jnp.logical_and(inplane, jnp.logical_or(column, via_x)), copy(0, k, c, x_dev, span)),
            (jnp.logical_and(inplane, jnp.logical_or(column, via_y)), copy(1, k, c, y_dev, span)),
        )

    def forward(k, c, dx, dy, szz, span):
        for condition, route in routes(k, c, dx, dy, szz, span):
            @pl.when(condition)
            def _():
                route.start()

    everything = pl.ds(0, rows)

    def item(q):
        r, i = q // 2, q % 2
        dx, dy = r % 2, r // 2
        first = jnp.where(zz >= 1, 1, 0)
        szz = first + i * (1 - 2 * first)
        src_z = szz + s * (DEPTH - 1 - 2 * szz)
        k = src_z * PLANE + ((y + dy) % 2) * 2 + (x + dx) % 2 - half_n * s
        return k, dx, dy, szz

    def send_own(c):
        @pl.when(jnp.logical_and(is_source, c < CHUNKS))
        def _():
            forward(own_k, c, 0, 0, zz, mine)
            pair_copy(own_k, c, theirs).wait_recv()
            forward(own_k, c, 0, 0, zz, theirs)

    def lead(c, carry):
        send_own(c)
        return carry

    lax.fori_loop(0, LEAD, lead, 0)
    load_w.wait()
    load_t.wait()

    def far_copy(c):
        return pltpu.make_async_remote_copy(
            src_ref=part.at[c],
            dst_ref=far.at[c],
            send_sem=far_sent.at[0],
            recv_sem=far_recv.at[c],
            device_id=pair_dev,
            device_id_type=MESH,
        )

    def stat_copy(c, core, d):
        return pltpu.make_async_remote_copy(
            src_ref=stats.at[c, 0],
            dst_ref=stats.at[c, d],
            send_sem=stat_sent.at[core],
            recv_sem=stat_recv.at[c],
            device_id=(core, (v + d) % n),
            device_id_type=MESH,
        )

    def local_stats(c):
        far_copy(c).wait_recv()

        both = part[c] + far[c]
        logits, slope = both[:, :width], both[:, width:]
        top = jnp.max(logits, axis=1, keepdims=True)
        e = jnp.exp(logits - top)
        amount = jnp.sum(e, axis=1, keepdims=True)
        weighted = jnp.sum(e * slope, axis=1, keepdims=True)
        columns = lax.broadcasted_iota(jnp.int32, logits.shape, 1) + v * width
        picked = jnp.sum(jnp.where(columns == wanted[c][:, 0:1], logits, 0.0), axis=1, keepdims=True)
        lane = lax.broadcasted_iota(jnp.int32, (rows, LANES), 1)
        packed = jnp.where(lane == 0, top, jnp.where(lane == 1, amount, jnp.where(lane == 2, weighted, picked)))
        stats[c, 0] = packed.T[:4]

        stat_copy(c, 1 - s, 0).start()

        def start(d, carry):
            stat_copy(c, 0, n - d).start()
            stat_copy(c, 1, n - d).start()
            return carry

        lax.fori_loop(1, n, start, 0)

    def finish(c):
        @pl.when(is_source)
        def _():
            far_copy(c).wait_recv()
            bulk(stats.at[c], stat_recv.at[c]).wait_recv()

        @pl.when(jnp.logical_not(is_source))
        def _():
            bulk(stats.at[c, pl.ds(1, n - 1)], stat_recv.at[c]).wait_recv()

        every = stats[c]
        tops = every[:, 0, :]
        row_top = jnp.max(tops, axis=0, keepdims=True)
        scale = jnp.exp(tops - row_top)
        totals = jnp.sum(scale * every[:, 1, :], axis=0, keepdims=True)
        tangent_sum = jnp.sum(scale * every[:, 2, :], axis=0, keepdims=True)
        picked = jnp.sum(every[:, 3, :], axis=0, keepdims=True)
        expect = tangent_sum / totals
        line = lax.broadcasted_iota(jnp.int32, (LANES, rows), 0)
        side = jnp.where(line == 0, row_top, jnp.where(line == 1, totals, expect)).T
        both = part[c] + far[c]
        value = jnp.exp(both[:, :width] - side[:, 0:1]) / side[:, 1:2] * (both[:, width:] - side[:, 2:3])
        term[c] = value.astype(term.dtype)
        loss = row_top + jnp.log(totals) - picked
        place = c % 2
        loss = jnp.where(place == s, loss, pltpu.roll(loss, half, 1))
        lane = lax.broadcasted_iota(jnp.int32, (1, rows), 1)
        kept = loss_out[c // 2]
        loss_out[c // 2] = jnp.where(lane // half == place, loss, kept)

    def product(g, k):
        left = flipped[k, :, pl.ds(pl.multiple_of(g * group_rows, group_rows), group_rows)]
        right = term[pl.ds(2 * g, 2)].reshape(group_rows, width)
        total[k] += jnp.dot(left, right, preferred_element_type=jnp.float32)

    def product_due(done):
        late = done - finish_lag - 2
        return jnp.logical_and(late >= 0, jnp.logical_and(late % 2 == 0, late < CHUNKS - 2)), late // 2

    def stages(done):
        @pl.when(jnp.logical_and(jnp.logical_not(is_source), jnp.logical_and(done >= 0, done < CHUNKS)))
        def _():
            local_stats(done)

        @pl.when(done >= finish_lag)
        def _():
            finish(done - finish_lag)

    def step(t, carry):
        done = t - last_lag

        @pl.when(t == 0)
        def _():
            pl.semaphore_wait(hello.at[0], 1)
            greet(hello.at[1], y_dev)

        @pl.when(t == 1)
        def _():
            pl.semaphore_wait(hello.at[1], 1)
            greet_along(hello.at[2])

        @pl.when(t == 2)
        def _():
            pair_target.wait()
            for g in range(GROUPS):
                for ids, side in ((target, mine), (target_pair, theirs)):
                    upright = jnp.broadcast_to(ids[:, g * rows : (g + 1) * rows], (LANES, rows)).T
                    wanted[2 * g, side, :] = upright[:half]
                    wanted[2 * g + 1, side, :] = upright[half:]

            pl.semaphore_wait(hello.at[2], along_count)
            greet_along(hello.at[3])

        @pl.when(t == 3)
        def _():
            pl.semaphore_wait(hello.at[3], along_count)
            greet_along(hello.at[4])

        send_own(t + LEAD)
        ready, g_ready = product_due(done)

        def one(i, inner):
            q = field(order_word, i, 3)
            c = t - field(lag_word, q, 4)

            @pl.when(jnp.logical_and(c >= 0, c < CHUNKS))
            def _():
                k, dx, dy, szz = item(q)
                own = jnp.logical_and(dx + dy == 0, szz == zz)

                @pl.when(jnp.logical_not(own))
                def _():
                    copy(0, k, c, x_dev, everything).wait_recv()
                    forward(k, c, dx, dy, szz, everything)

                piece = hid[k * CHUNKS + c]
                part[c, :, :width] += jnp.dot(piece, wv[k], preferred_element_type=jnp.float32)
                part[c, :, width:] += jnp.dot(piece, tv[k], preferred_element_type=jnp.float32)

                @pl.when(c < CHUNKS - 2)
                def _():
                    flipped[k, :, pl.ds(pl.multiple_of(c * rows, rows), rows)] = hid[k * CHUNKS + c].T

                @pl.when(c >= CHUNKS - 2)
                def _():
                    at = (c - CHUNKS + 2) * rows
                    last[k, :, pl.ds(pl.multiple_of(at, rows), rows)] = hid[k * CHUNKS + c].T

            @pl.when(ready)
            def _():
                product(g_ready, i)

            return inner

        lax.fori_loop(0, 8, one, 0)

        @pl.when(done == 0)
        def _():
            pl.semaphore_wait(hello.at[4], along_count)

        @pl.when(done >= 0)
        def _():
            far_copy(done).start()

        stages(done)
        return carry

    lax.fori_loop(0, CHUNKS + last_lag, step, 0)

    def after(done, carry):
        stages(done)
        ready, g_ready = product_due(done)

        @pl.when(ready)
        def _():
            def one(k, inner):
                product(g_ready, k)
                return inner

            lax.fori_loop(0, half_n, one, 0)

        return carry

    lax.fori_loop(CHUNKS, CHUNKS + finish_lag - 1, after, 0)

    corners = [links_used(i // 4, i // 2 % 2, i % 2) for i in range(4 * DEPTH)]
    corner = zz * 4 + y * 2 + x
    for link in range(4):
        counts = [used[link] for used in corners]
        used = pick(corner, counts)
        for count in sorted(set(counts) - {0}):

            @pl.when(used == count)
            def _():
                bulk(hid.at[pl.ds(0, count)], sent.at[link]).wait_send()

    bulk(part, far_sent.at[0]).wait_send()

    @pl.when(jnp.logical_not(is_source))
    def _():
        bulk(staged, pair_sent.at[0]).wait_send()
        bulk(stats.at[:, pl.ds(1, n - 1)], stat_sent.at[s]).wait_send()
        bulk(stats, stat_sent.at[1 - s]).wait_send()

    finish(CHUNKS - 1)


def product_kernel(total, last, term, loss_in, out, loss_out, rounded, sem):
    half_n = total.shape[0]
    right = term[pl.ds(CHUNKS - 2, 2)].reshape(last.shape[2], term.shape[2])

    def copy(k):
        return pltpu.make_async_copy(rounded.at[k], out.at[k], sem.at[k])

    def one(k, carry):
        rounded[k] = (total[k] + jnp.dot(last[k], right, preferred_element_type=jnp.float32)).astype(out.dtype)
        copy(k).start()
        return carry

    lax.fori_loop(0, half_n, one, 0)
    for g in range(GROUPS):
        loss_out[g * LANES : (g + 1) * LANES] = loss_in[g, 0]

    def settle(k, carry):
        copy(k).wait()
        return carry

    lax.fori_loop(0, half_n, settle, 0)


def relayed(n, hidden, weight, tangent, targets):
    half_n = n // 2
    tokens_own, shard = hidden.shape
    width = weight.shape[1]
    rows = 2 * tokens_own // CHUNKS
    blocks = (half_n, shard, width)
    hbm = pl.BlockSpec(memory_space=pltpu.HBM)
    vmem = pl.BlockSpec(memory_space=pltpu.VMEM)
    dma = pltpu.SemaphoreType.DMA
    total, last, term, loss = pl.pallas_call(
        functools.partial(gather_kernel, n),
        name="gather_logits",
        out_shape=(
            pltpu.VMEM(blocks, jnp.float32),
            pltpu.VMEM((half_n, shard, 2 * rows), hidden.dtype),
            pltpu.VMEM((CHUNKS, rows, width), jnp.bfloat16),
            pltpu.VMEM((GROUPS, 1, rows), jnp.float32),
        ),
        in_specs=[hbm, hbm, hbm, hbm],
        out_specs=(vmem, vmem, vmem, vmem),
        scratch_shapes=[
            pltpu.VMEM((half_n * CHUNKS, rows, shard), hidden.dtype),
            pltpu.VMEM((half_n, shard, (CHUNKS - 2) * rows), hidden.dtype),
            pltpu.VMEM((CHUNKS, rows // 2, shard), hidden.dtype),
            pltpu.VMEM(blocks, weight.dtype),
            pltpu.VMEM(blocks, tangent.dtype),
            pltpu.VMEM((CHUNKS, rows, 2 * width), jnp.float32),
            pltpu.VMEM((CHUNKS, rows, 2 * width), jnp.float32),
            pltpu.VMEM((CHUNKS, n, 4, rows), jnp.float32),
            pltpu.VMEM((1, tokens_own), jnp.int32),
            pltpu.VMEM((1, tokens_own), jnp.int32),
            pltpu.VMEM((CHUNKS, rows, LANES), jnp.int32),
            dma((half_n, CHUNKS)),
            dma((4,)),
            dma((CHUNKS,)),
            dma((1,)),
            dma((4,)),
            dma((1,)),
            dma((CHUNKS,)),
            dma((2,)),
            dma((CHUNKS,)),
            dma((2,)),
            pltpu.SemaphoreType.REGULAR((5,)),
        ],
        compiler_params=pltpu.CompilerParams(
            collective_id=0, has_side_effects=True, vmem_limit_bytes=42 * 2**20
        ),
    )(
        pltpu.with_memory_space_constraint(hidden.reshape(CHUNKS, rows // 2, shard), pltpu.HBM),
        pltpu.with_memory_space_constraint(weight.reshape(blocks), pltpu.HBM),
        pltpu.with_memory_space_constraint(tangent.reshape(blocks), pltpu.HBM),
        pltpu.with_memory_space_constraint(targets.reshape(1, tokens_own), pltpu.HBM),
    )
    ggn, token_loss = pl.pallas_call(
        product_kernel,
        name="product",
        out_shape=(
            jax.ShapeDtypeStruct(blocks, jnp.bfloat16),
            jax.ShapeDtypeStruct((tokens_own,), jnp.float32),
        ),
        in_specs=[vmem, vmem, vmem, vmem],
        out_specs=(hbm, vmem),
        scratch_shapes=[pltpu.VMEM(blocks, jnp.bfloat16), dma((half_n,))],
        compiler_params=pltpu.CompilerParams(vmem_limit_bytes=20 * 2**20),
    )(total, last, term, loss)
    return ggn.reshape(weight.shape), token_loss


def partner(value, axis, stride):
    mask = 2**stride
    pairs = [(source, source ^ mask) for source in range(lax.axis_size(axis))]
    return lax.ppermute(value, axis, pairs)


def on_device(hidden, weight, tangent, targets):
    n = lax.axis_size("vocab")
    if n == PLANE * DEPTH and lax.axis_size("seq") == 2 and hidden.shape[0] == LANES * GROUPS and hidden.shape[1] % LANES == 0:
        return relayed(n, hidden, weight, tangent, targets)
    vocab_index = lax.axis_index("vocab")
    shard_width = weight.shape[1]
    half_width = weight.shape[0]
    whole = lax.all_gather(hidden, "vocab", axis=1, tiled=True)
    seq_index = lax.axis_index("seq")
    own_part = lax.dynamic_slice_in_dim(whole, seq_index * half_width, half_width, 1)
    far_part = lax.dynamic_slice_in_dim(whole, (1 - seq_index) * half_width, half_width, 1)
    received = partner(far_part, "seq", 0)
    leading = jnp.where(seq_index == 0, own_part, received)
    trailing = jnp.where(seq_index == 0, received, own_part)
    stacked = jnp.concatenate([leading, trailing], axis=0)
    partial_logits = jnp.dot(stacked, weight, preferred_element_type=jnp.float32)
    partial_tangent = jnp.dot(stacked, tangent, preferred_element_type=jnp.float32)
    logits, tangent_logits = (
        lax.psum_scatter(partial_logits, "seq", scatter_dimension=0, tiled=True),
        lax.psum_scatter(partial_tangent, "seq", scatter_dimension=0, tiled=True),
    )
    local_target = targets - vocab_index * shard_width
    columns_ids = jnp.arange(shard_width, dtype=jnp.int32)
    picked_local = jnp.sum(
        jnp.where(columns_ids[None, :] == local_target[:, None], logits, jnp.float32(0.0)), axis=1
    )
    local_top = jnp.max(logits, axis=1)
    row_top = lax.pmax(local_top, "vocab")
    exp_logits = jnp.exp(logits - row_top[:, None])
    totals, tangent_sum, picked = lax.psum(
        (jnp.sum(exp_logits, axis=1), jnp.sum(exp_logits * tangent_logits, axis=1), picked_local),
        "vocab",
    )
    expect = tangent_sum / totals
    token_loss = row_top + jnp.log(totals) - picked
    weight_term = (exp_logits / totals[:, None] * (tangent_logits - expect[:, None])).astype(
        jnp.bfloat16
    )
    far_term = partner(weight_term, "seq", 0)
    lead_term = jnp.where(seq_index == 0, weight_term, far_term)
    trail_term = jnp.where(seq_index == 0, far_term, weight_term)
    all_terms = jnp.concatenate([lead_term, trail_term], axis=0)
    ggn = jnp.einsum("td,tv->dv", stacked, all_terms, preferred_element_type=jnp.float32).astype(
        jnp.bfloat16
    )
    return (ggn, token_loss)


def solution(mesh):
    in_specs = (P("seq", "vocab"), P("seq", "vocab"), P("seq", "vocab"), P("seq"))
    out_specs = (P("seq", "vocab"), P("seq"))
    return jax.shard_map(
        on_device, mesh=mesh, in_specs=in_specs, out_specs=out_specs, check_vma=False
    )
```

time: 96.1 us -> 89.6 us (0.932)
  Pallas kernels: 94.7 us -> 88.8 us
    pallas_call x1, Pallas kernels: 8.74 us -> 3.88 us  [relayed(): pl.pallas_call(product_kernel, name='product', out_shape=(jax.ShapeDtypeS...]
    pallas_call x1, Pallas kernels: 85.9 us -> 84.9 us  [relayed(): pl.pallas_call(functools.partial(gather_kernel, n), name='gather_logits',...]
where the time goes in v1:
time: 89.6 us; the launch traced here: 89.5 us
  Pallas kernels  88.8 us (99%)
    pallas_call x1, Pallas kernels, relayed(): pl.pallas_call(functools.partial(gather_kernel, n), name='gather_logits',...  84.9 us
    pallas_call x1, Pallas kernels, relayed(): pl.pallas_call(product_kernel, name='product', out_shape=(jax.ShapeDtypeS...  3.88 us

profile of v1, /device:TPU:0, one launch (start us, length us, event | category | flops | bytes accessed | tf_op | source)
XLA Modules:
  0.0 89.5 jit_solution(11761705042840510795)
XLA Ops:
  0.6 84.9 %gather_logits.1 = (f32[8,512,512]{2,1,0:T(8,128)S(1)}, bf16[8,512,256]{2,1,0:T(8,128)(2,1)S(1)}, bf16[8,128,512]{2,1,0:T(8,128)(2,1)S(1)}, f32[4,1,128]{2,1,0:T(1,128)S(1)}) custom-call(bf16[8,64,512]{2,1,0:T(8,128)(2,1)} %bitcast.7, bf16[8,512,512]{2,1,0:T(8,128)(2,1)} %bitcast.5, bf16[8,512,512]{2,1,0:T(8,128)(2,1)} %bitcast.6, s32[1,512]{1,0:T(1,128)} %bitcast.8), custom_call_target="tpu_custom_call" | custom-call | tf_op jit(solution)/shard_map/gather_logits/pallas_call | solution.py:492
  85.6 3.9 %product.1 = (bf16[8,512,512]{2,1,0:T(8,128)(2,1)}, f32[512]{0:T(512)}) custom-call(f32[8,512,512]{2,1,0:T(8,128)S(1)} %get-tuple-element.8.total, bf16[8,512,256]{2,1,0:T(8,128)(2,1)S(1)} %get-tuple-element.9.last, bf16[8,128,512]{2,1,0:T(8,128)(2,1)S(1)} %get-tuple-element.10.term, f32[4,1,128]{2,1,0:T(1,128)S(1)} %get-tuple-element.11.loss_in), custom_call_target="tpu_custom_call" | custom-call | tf_op jit(solution)/shard_map/product/pallas_call | solution.py:536

commit v2 on v1

--- a/solution.py
+++ b/solution.py
@@ -12,11 +12,12 @@
 CHUNKS = 8
 GROUPS = CHUNKS // 2
 LEAD = 3
-LAGS = ((0, 0, 2, 2, 2, 2, 4, 4), (0, 0, 2, 2, 2, 2, 4, 4), (0, 0, 2, 2, 2, 2, 4, 4), (0, 0, 2, 2, 2, 2, 4, 4))
-ORDERS = ((0, 1, 2, 3, 4, 5, 6, 7), (0, 1, 2, 3, 4, 5, 6, 7), (0, 1, 2, 3, 4, 5, 6, 7), (0, 1, 2, 3, 4, 5, 6, 7))
-TALL = (0, 0, 0, 255, 0, 0, 0, 0)
-DEEP = (0, 0, 0, 15, 0, 0, 0, 0)
-VIA = (0, 255, 0, 255, 255, 0, 255, 0)
+LAGS = ((0, 0, 0, 3, 0, 2, 1, 5), (0, 1, 1, 3, 3, 4, 4, 5), (0, 0, 2, 2, 2, 3, 4, 5), (0, 0, 2, 2, 2, 3, 5, 5))
+ORDERS = ((5, 2, 7, 4, 1, 3, 6, 0), (5, 3, 0, 4, 1, 6, 7, 2), (5, 0, 2, 4, 7, 1, 6, 3), (6, 5, 7, 2, 0, 3, 1, 4))
+TALL = (78, 18, 144, 0, 129, 44, 176, 224)
+DEEP = (4, 0, 1, 1, 0, 0, 0, 0)
+VIA = (30, 12, 167, 159, 99, 142, 22, 95)
+FINISH_LAGS = (8, 8, 4, 4)
 LANES = 128
 
 
@@ -56,9 +57,9 @@
 
 def gather_kernel(
     n, hidden, weight, tangent, targets, total, last, term, loss_out,
-    hid, flipped, staged, wv, tv, part, far, stats, target, target_pair, wanted,
+    hid, flipped, staged, both_w, part, far, stats, target, target_pair, wanted,
     recv, sent, pair_recv, pair_sent, load_sem, far_sent, far_recv,
-    stat_sent, stat_recv, target_sem, hello,
+    stat_sent, stat_recv, target_sem,
 ):
     s = lax.axis_index("seq")
     v = lax.axis_index("vocab")
@@ -66,7 +67,7 @@
     rows = hid.shape[1]
     half = rows // 2
     group_rows = 2 * rows
-    width = wv.shape[2]
+    width = weight.shape[2]
     z, y, x = v // PLANE, (v // 2) % 2, v % 2
     zz = z + s * (DEPTH - 1 - 2 * z)
     up_step = PLANE * (1 - 2 * s)
@@ -84,13 +85,13 @@
     lag_word = pick(zz, [packed(lags, 4) for lags in LAGS])
     order_word = pick(zz, [packed(order, 3) for order in ORDERS])
     last_lag = pick(zz, [max(lags) for lags in LAGS])
-    finish_lag = jnp.where(is_source, 4, 2)
+    finish_lag = pick(zz, FINISH_LAGS)
 
     mine = pl.ds(pl.multiple_of(s * half, half), half)
     theirs = pl.ds(pl.multiple_of((1 - s) * half, half), half)
 
-    load_w = pltpu.make_async_copy(weight, wv, load_sem.at[0])
-    load_t = pltpu.make_async_copy(tangent, tv, load_sem.at[1])
+    load_w = pltpu.make_async_copy(weight, both_w.at[:, :, pl.ds(0, width)], load_sem.at[0])
+    load_t = pltpu.make_async_copy(tangent, both_w.at[:, :, pl.ds(width, width)], load_sem.at[1])
     load_target = pltpu.make_async_copy(targets, target, load_sem.at[2])
 
     own_load = pltpu.make_async_copy(hidden, hid.at[pl.ds(own_k * CHUNKS, CHUNKS), mine], load_sem.at[3])
@@ -148,14 +149,12 @@
 
     def clear(i, carry):
         part[i] = jnp.zeros(part.shape[1:], jnp.float32)
-        total[i] = jnp.zeros(total.shape[1:], jnp.float32)
         return carry
 
     lax.fori_loop(0, CHUNKS, clear, 0)
     loss_out[...] = jnp.zeros_like(loss_out)
     load_target.wait()
     pl.semaphore_wait(barrier, 3 + along_count)
-    greet(hello.at[0], x_dev)
     pair_target = pltpu.make_async_remote_copy(
         src_ref=target,
         dst_ref=target_pair,
@@ -243,6 +242,17 @@
         return carry
 
     lax.fori_loop(0, LEAD, lead, 0)
+
+    pair_target.wait()
+
+    @pl.when(jnp.logical_not(is_source))
+    def _():
+        for g in range(GROUPS):
+            for ids, side in ((target, mine), (target_pair, theirs)):
+                upright = jnp.broadcast_to(ids[:, g * rows : (g + 1) * rows], (LANES, rows)).T
+                wanted[2 * g, side, :] = upright[:half]
+                wanted[2 * g + 1, side, :] = upright[half:]
+
     load_w.wait()
     load_t.wait()
 
@@ -320,56 +330,48 @@
         kept = loss_out[c // 2]
         loss_out[c // 2] = jnp.where(lane // half == place, loss, kept)
 
-    def product(g, k):
-        left = flipped[k, :, pl.ds(pl.multiple_of(g * group_rows, group_rows), group_rows)]
-        right = term[pl.ds(2 * g, 2)].reshape(group_rows, width)
-        total[k] += jnp.dot(left, right, preferred_element_type=jnp.float32)
+    early = 2 * group_rows
+
+    def product(first, second, k):
+        @pl.when(first)
+        def _():
+            right = term[pl.ds(0, 4)].reshape(early, width)
+            total[k] = jnp.dot(flipped[k, :, pl.ds(0, early)], right, preferred_element_type=jnp.float32)
+
+        @pl.when(second)
+        def _():
+            right = term[pl.ds(4, 2)].reshape(group_rows, width)
+            left = flipped[k, :, pl.ds(early, group_rows)]
+            total[k] += jnp.dot(left, right, preferred_element_type=jnp.float32)
 
     def product_due(done):
-        late = done - finish_lag - 2
-        return jnp.logical_and(late >= 0, jnp.logical_and(late % 2 == 0, late < CHUNKS - 2)), late // 2
+        return done == finish_lag + 4, done == finish_lag + 6
+
+    def ripe(done, act):
+        single = done >= CHUNKS - 2
+        whole = jnp.logical_and(done >= 0, done % 2 == 1)
+        valid = jnp.logical_and(done < CHUNKS, jnp.logical_or(single, whole))
+
+        def one(c, carry):
+            act(c)
+            return carry
+
+        @pl.when(valid)
+        def _():
+            lax.fori_loop(jnp.where(single, done, done - 1), done + 1, one, 0)
 
     def stages(done):
-        @pl.when(jnp.logical_and(jnp.logical_not(is_source), jnp.logical_and(done >= 0, done < CHUNKS)))
-        def _():
-            local_stats(done)
-
-        @pl.when(done >= finish_lag)
-        def _():
-            finish(done - finish_lag)
+        @pl.when(jnp.logical_not(is_source))
+        def _():
+            ripe(done, local_stats)
+
+        ripe(done - finish_lag, finish)
 
     def step(t, carry):
         done = t - last_lag
 
-        @pl.when(t == 0)
-        def _():
-            pl.semaphore_wait(hello.at[0], 1)
-            greet(hello.at[1], y_dev)
-
-        @pl.when(t == 1)
-        def _():
-            pl.semaphore_wait(hello.at[1], 1)
-            greet_along(hello.at[2])
-
-        @pl.when(t == 2)
-        def _():
-            pair_target.wait()
-            for g in range(GROUPS):
-                for ids, side in ((target, mine), (target_pair, theirs)):
-                    upright = jnp.broadcast_to(ids[:, g * rows : (g + 1) * rows], (LANES, rows)).T
-                    wanted[2 * g, side, :] = upright[:half]
-                    wanted[2 * g + 1, side, :] = upright[half:]
-
-            pl.semaphore_wait(hello.at[2], along_count)
-            greet_along(hello.at[3])
-
-        @pl.when(t == 3)
-        def _():
-            pl.semaphore_wait(hello.at[3], along_count)
-            greet_along(hello.at[4])
-
         send_own(t + LEAD)
-        ready, g_ready = product_due(done)
+        first, second = product_due(done)
 
         def one(i, inner):
             q = field(order_word, i, 3)
@@ -385,35 +387,25 @@
                     copy(0, k, c, x_dev, everything).wait_recv()
                     forward(k, c, dx, dy, szz, everything)
 
-                piece = hid[k * CHUNKS + c]
-                part[c, :, :width] += jnp.dot(piece, wv[k], preferred_element_type=jnp.float32)
-                part[c, :, width:] += jnp.dot(piece, tv[k], preferred_element_type=jnp.float32)
-
-                @pl.when(c < CHUNKS - 2)
+                @pl.when(jnp.logical_and(c < CHUNKS - 2, c % 2 == 1))
                 def _():
-                    flipped[k, :, pl.ds(pl.multiple_of(c * rows, rows), rows)] = hid[k * CHUNKS + c].T
+                    two = hid[pl.ds(k * CHUNKS + c - 1, 2)].reshape(group_rows, hid.shape[2])
+                    more = jnp.dot(two, both_w[k], preferred_element_type=jnp.float32)
+                    part[pl.ds(c - 1, 2)] += more.reshape(2, rows, 2 * width)
+                    flipped[k, :, pl.ds(pl.multiple_of((c - 1) * rows, group_rows), group_rows)] = two.T
 
                 @pl.when(c >= CHUNKS - 2)
                 def _():
+                    part[c] += jnp.dot(hid[k * CHUNKS + c], both_w[k], preferred_element_type=jnp.float32)
                     at = (c - CHUNKS + 2) * rows
                     last[k, :, pl.ds(pl.multiple_of(at, rows), rows)] = hid[k * CHUNKS + c].T
 
-            @pl.when(ready)
-            def _():
-                product(g_ready, i)
-
+            product(first, second, i)
             return inner
 
         lax.fori_loop(0, 8, one, 0)
 
-        @pl.when(done == 0)
-        def _():
-            pl.semaphore_wait(hello.at[4], along_count)
-
-        @pl.when(done >= 0)
-        def _():
-            far_copy(done).start()
-
+        ripe(done, lambda c: far_copy(c).start())
         stages(done)
         return carry
 
@@ -421,12 +413,12 @@
 
     def after(done, carry):
         stages(done)
-        ready, g_ready = product_due(done)
-
-        @pl.when(ready)
+        first, second = product_due(done)
+
+        @pl.when(jnp.logical_or(first, second))
         def _():
             def one(k, inner):
-                product(g_ready, k)
+                product(first, second, k)
                 return inner
 
             lax.fori_loop(0, half_n, one, 0)
@@ -469,7 +461,7 @@
         copy(k).start()
         return carry
 
-    lax.fori_loop(0, half_n, one, 0)
+    lax.fori_loop(0, half_n, one, 0, unroll=4)
     for g in range(GROUPS):
         loss_out[g * LANES : (g + 1) * LANES] = loss_in[g, 0]
 
@@ -504,8 +496,7 @@
             pltpu.VMEM((half_n * CHUNKS, rows, shard), hidden.dtype),
             pltpu.VMEM((half_n, shard, (CHUNKS - 2) * rows), hidden.dtype),
             pltpu.VMEM((CHUNKS, rows // 2, shard), hidden.dtype),
-            pltpu.VMEM(blocks, weight.dtype),
-            pltpu.VMEM(blocks, tangent.dtype),
+            pltpu.VMEM((half_n, shard, 2 * width), weight.dtype),
             pltpu.VMEM((CHUNKS, rows, 2 * width), jnp.float32),
             pltpu.VMEM((CHUNKS, rows, 2 * width), jnp.float32),
             pltpu.VMEM((CHUNKS, n, 4, rows), jnp.float32),
@@ -522,7 +513,6 @@
             dma((2,)),
             dma((CHUNKS,)),
             dma((2,)),
-            pltpu.SemaphoreType.REGULAR((5,)),
         ],
         compiler_params=pltpu.CompilerParams(
             collective_id=0, has_side_effects=True, vmem_limit_bytes=42 * 2**20

time: 89.6 us -> 83.1 us (0.927)
  Pallas kernels: 88.8 us -> 82.3 us
    pallas_call x1, Pallas kernels: 84.9 us -> 79.3 us  [relayed(): pl.pallas_call(functools.partial(gather_kernel, n), name='gather_logits',...]
where the time goes in v2:
time: 83.1 us; the launch traced here: 83 us
  Pallas kernels  82.3 us (99%)
    pallas_call x1, Pallas kernels, relayed(): pl.pallas_call(functools.partial(gather_kernel, n), name='gather_logits',...  79.3 us
    pallas_call x1, Pallas kernels, relayed(): pl.pallas_call(product_kernel, name='product', out_shape=(jax.ShapeDtypeS...  3.02 us

profile of v2, /device:TPU:0, one launch (start us, length us, event | category | flops | bytes accessed | tf_op | source)
XLA Modules:
  0.0 83.0 jit_solution(11009851442678387116)
XLA Ops:
  0.6 79.3 %gather_logits.1 = (f32[8,512,512]{2,1,0:T(8,128)S(1)}, bf16[8,512,256]{2,1,0:T(8,128)(2,1)S(1)}, bf16[8,128,512]{2,1,0:T(8,128)(2,1)S(1)}, f32[4,1,128]{2,1,0:T(1,128)S(1)}) custom-call(bf16[8,64,512]{2,1,0:T(8,128)(2,1)} %bitcast.7, bf16[8,512,512]{2,1,0:T(8,128)(2,1)} %bitcast.5, bf16[8,512,512]{2,1,0:T(8,128)(2,1)} %bitcast.6, s32[1,512]{1,0:T(1,128)} %bitcast.8), custom_call_target="tpu_custom_call" | custom-call | tf_op jit(solution)/shard_map/gather_logits/pallas_call | solution.py:484
  80.0 3.0 %product.1 = (bf16[8,512,512]{2,1,0:T(8,128)(2,1)}, f32[512]{0:T(512)}) custom-call(f32[8,512,512]{2,1,0:T(8,128)S(1)} %get-tuple-element.8.total, bf16[8,512,256]{2,1,0:T(8,128)(2,1)S(1)} %get-tuple-element.9.last, bf16[8,128,512]{2,1,0:T(8,128)(2,1)S(1)} %get-tuple-element.10.term, f32[4,1,128]{2,1,0:T(1,128)S(1)} %get-tuple-element.11.loss_in), custom_call_target="tpu_custom_call" | custom-call | tf_op jit(solution)/shard_map/product/pallas_call | solution.py:526

commit v3 on v2

--- a/solution.py
+++ b/solution.py
@@ -11,14 +11,16 @@
 PLANE, DEPTH = 4, 4
 CHUNKS = 8
 GROUPS = CHUNKS // 2
-LEAD = 3
-LAGS = ((0, 0, 0, 3, 0, 2, 1, 5), (0, 1, 1, 3, 3, 4, 4, 5), (0, 0, 2, 2, 2, 3, 4, 5), (0, 0, 2, 2, 2, 3, 5, 5))
-ORDERS = ((5, 2, 7, 4, 1, 3, 6, 0), (5, 3, 0, 4, 1, 6, 7, 2), (5, 0, 2, 4, 7, 1, 6, 3), (6, 5, 7, 2, 0, 3, 1, 4))
-TALL = (78, 18, 144, 0, 129, 44, 176, 224)
-DEEP = (4, 0, 1, 1, 0, 0, 0, 0)
-VIA = (30, 12, 167, 159, 99, 142, 22, 95)
-FINISH_LAGS = (8, 8, 4, 4)
+LEAD = 4
+LAGS = ((0, 0, 1, 4, 0, 3, 4, 5), (0, 0, 1, 3, 1, 3, 4, 5), (0, 0, 2, 2, 2, 3, 5, 5), (0, 0, 2, 3, 3, 3, 5, 5))
+ORDERS = ((5, 0, 6, 3, 4, 1, 7, 2), (0, 3, 2, 5, 4, 6, 1, 7), (6, 5, 0, 1, 4, 7, 2, 3), (4, 5, 3, 0, 2, 6, 7, 1))
+TALL = (156, 62, 1, 4, 8, 40, 67, 72)
+DEEP = (4, 0, 0, 1, 0, 0, 0, 0)
+VIA = (133, 200, 63, 62, 116, 28, 123, 1)
+FINISH_LAG = 4
+FINISHED = (CHUNKS - FINISH_LAG) // 2
 LANES = 128
+UNROLL = 4
 
 
 def links_used(zz, y, x):
@@ -85,7 +87,6 @@
     lag_word = pick(zz, [packed(lags, 4) for lags in LAGS])
     order_word = pick(zz, [packed(order, 3) for order in ORDERS])
     last_lag = pick(zz, [max(lags) for lags in LAGS])
-    finish_lag = pick(zz, FINISH_LAGS)
 
     mine = pl.ds(pl.multiple_of(s * half, half), half)
     theirs = pl.ds(pl.multiple_of((1 - s) * half, half), half)
@@ -152,7 +153,6 @@
         return carry
 
     lax.fori_loop(0, CHUNKS, clear, 0)
-    loss_out[...] = jnp.zeros_like(loss_out)
     load_target.wait()
     pl.semaphore_wait(barrier, 3 + along_count)
     pair_target = pltpu.make_async_remote_copy(
@@ -256,61 +256,63 @@
     load_w.wait()
     load_t.wait()
 
-    def far_copy(c):
+    def far_copy(g):
         return pltpu.make_async_remote_copy(
-            src_ref=part.at[c],
-            dst_ref=far.at[c],
+            src_ref=part.at[pl.ds(2 * g, 2)],
+            dst_ref=far.at[pl.ds(2 * g, 2)],
             send_sem=far_sent.at[0],
-            recv_sem=far_recv.at[c],
+            recv_sem=far_recv.at[g],
             device_id=pair_dev,
             device_id_type=MESH,
         )
 
-    def stat_copy(c, core, d):
+    def stat_copy(g, core, d):
         return pltpu.make_async_remote_copy(
-            src_ref=stats.at[c, 0],
-            dst_ref=stats.at[c, d],
+            src_ref=stats.at[g, 0],
+            dst_ref=stats.at[g, d],
             send_sem=stat_sent.at[core],
-            recv_sem=stat_recv.at[c],
-            device_id=(core, (v + d) % n),
+            recv_sem=stat_recv.at[g],
+            device_id=(core, v ^ d),
             device_id_type=MESH,
         )
 
-    def local_stats(c):
-        far_copy(c).wait_recv()
-
-        both = part[c] + far[c]
+    def sums(g):
+        return (part[pl.ds(2 * g, 2)] + far[pl.ds(2 * g, 2)]).reshape(group_rows, 2 * width)
+
+    def local_stats(g):
+        far_copy(g).wait_recv()
+        both = sums(g)
         logits, slope = both[:, :width], both[:, width:]
         top = jnp.max(logits, axis=1, keepdims=True)
         e = jnp.exp(logits - top)
         amount = jnp.sum(e, axis=1, keepdims=True)
         weighted = jnp.sum(e * slope, axis=1, keepdims=True)
         columns = lax.broadcasted_iota(jnp.int32, logits.shape, 1) + v * width
-        picked = jnp.sum(jnp.where(columns == wanted[c][:, 0:1], logits, 0.0), axis=1, keepdims=True)
-        lane = lax.broadcasted_iota(jnp.int32, (rows, LANES), 1)
+        ids = wanted[pl.ds(2 * g, 2)].reshape(group_rows, LANES)[:, 0:1]
+        picked = jnp.sum(jnp.where(columns == ids, logits, 0.0), axis=1, keepdims=True)
+        lane = lax.broadcasted_iota(jnp.int32, (group_rows, LANES), 1)
         packed = jnp.where(lane == 0, top, jnp.where(lane == 1, amount, jnp.where(lane == 2, weighted, picked)))
-        stats[c, 0] = packed.T[:4]
-
-        stat_copy(c, 1 - s, 0).start()
+        stats[g, 0] = packed.T[:4]
+        stat_copy(g, 1 - s, 0).start()
 
         def start(d, carry):
-            stat_copy(c, 0, n - d).start()
-            stat_copy(c, 1, n - d).start()
+            stat_copy(g, 0, n - d).start()
+            stat_copy(g, 1, n - d).start()
             return carry
 
         lax.fori_loop(1, n, start, 0)
 
-    def finish(c):
+    def finish(g):
         @pl.when(is_source)
         def _():
-            far_copy(c).wait_recv()
-            bulk(stats.at[c], stat_recv.at[c]).wait_recv()
+            far_copy(g).wait_recv()
+            bulk(stats.at[g], stat_recv.at[g]).wait_recv()
 
         @pl.when(jnp.logical_not(is_source))
         def _():
-            bulk(stats.at[c, pl.ds(1, n - 1)], stat_recv.at[c]).wait_recv()
-
-        every = stats[c]
+            bulk(stats.at[g, pl.ds(1, n - 1)], stat_recv.at[g]).wait_recv()
+
+        every = stats[g]
         tops = every[:, 0, :]
         row_top = jnp.max(tops, axis=0, keepdims=True)
         scale = jnp.exp(tops - row_top)
@@ -318,61 +320,55 @@
         tangent_sum = jnp.sum(scale * every[:, 2, :], axis=0, keepdims=True)
         picked = jnp.sum(every[:, 3, :], axis=0, keepdims=True)
         expect = tangent_sum / totals
-        line = lax.broadcasted_iota(jnp.int32, (LANES, rows), 0)
+        line = lax.broadcasted_iota(jnp.int32, (LANES, group_rows), 0)
         side = jnp.where(line == 0, row_top, jnp.where(line == 1, totals, expect)).T
-        both = part[c] + far[c]
+        both = sums(g)
         value = jnp.exp(both[:, :width] - side[:, 0:1]) / side[:, 1:2] * (both[:, width:] - side[:, 2:3])
-        term[c] = value.astype(term.dtype)
+        term[pl.ds(2 * g, 2)] = value.astype(term.dtype).reshape(2, rows, width)
         loss = row_top + jnp.log(totals) - picked
-        place = c % 2
-        loss = jnp.where(place == s, loss, pltpu.roll(loss, half, 1))
+        low, high = loss[:, :rows], loss[:, rows:]
+        low = jnp.where(s == 0, low, pltpu.roll(low, half, 1))
+        high = jnp.where(s == 1, high, pltpu.roll(high, half, 1))
         lane = lax.broadcasted_iota(jnp.int32, (1, rows), 1)
-        kept = loss_out[c // 2]
-        loss_out[c // 2] = jnp.where(lane // half == place, loss, kept)
+        loss_out[g] = jnp.where(lane < half, low, high)
 
     early = 2 * group_rows
 
-    def product(first, second, k):
-        @pl.when(first)
-        def _():
-            right = term[pl.ds(0, 4)].reshape(early, width)
+    def first_product():
+        right = term[pl.ds(0, 4)].reshape(early, width)
+
+        def one(k, carry):
             total[k] = jnp.dot(flipped[k, :, pl.ds(0, early)], right, preferred_element_type=jnp.float32)
-
-        @pl.when(second)
-        def _():
-            right = term[pl.ds(4, 2)].reshape(group_rows, width)
+            return carry
+
+        lax.fori_loop(0, half_n, one, 0, unroll=UNROLL)
+
+    def second_product():
+        right = term[pl.ds(4, 2)].reshape(group_rows, width)
+
+        def one(k, carry):
             left = flipped[k, :, pl.ds(early, group_rows)]
             total[k] += jnp.dot(left, right, preferred_element_type=jnp.float32)
-
-    def product_due(done):
-        return done == finish_lag + 4, done == finish_lag + 6
+            return carry
+
+        lax.fori_loop(0, half_n, one, 0, unroll=UNROLL)
 
     def ripe(done, act):
-        single = done >= CHUNKS - 2
-        whole = jnp.logical_and(done >= 0, done % 2 == 1)
-        valid = jnp.logical_and(done < CHUNKS, jnp.logical_or(single, whole))
-
-        def one(c, carry):
-            act(c)
-            return carry
-
-        @pl.when(valid)
-        def _():
-            lax.fori_loop(jnp.where(single, done, done - 1), done + 1, one, 0)
+        @pl.when(jnp.logical_and(done >= 0, done % 2 == 1))
+        def _():
+            act(done // 2)
 
     def stages(done):
         @pl.when(jnp.logical_not(is_source))
         def _():
             ripe(done, local_stats)
 
-        ripe(done - finish_lag, finish)
+            ripe(done - FINISH_LAG, finish)
 
     def step(t, carry):
         done = t - last_lag
 
         send_own(t + LEAD)
-        first, second = product_due(done)
-
         def one(i, inner):
             q = field(order_word, i, 3)
             c = t - field(lag_word, q, 4)
@@ -387,45 +383,38 @@
                     copy(0, k, c, x_dev, everything).wait_recv()
                     forward(k, c, dx, dy, szz, everything)
 
-                @pl.when(jnp.logical_and(c < CHUNKS - 2, c % 2 == 1))
+                @pl.when(c % 2 == 1)
                 def _():
                     two = hid[pl.ds(k * CHUNKS + c - 1, 2)].reshape(group_rows, hid.shape[2])
                     more = jnp.dot(two, both_w[k], preferred_element_type=jnp.float32)
                     part[pl.ds(c - 1, 2)] += more.reshape(2, rows, 2 * width)
-                    flipped[k, :, pl.ds(pl.multiple_of((c - 1) * rows, group_rows), group_rows)] = two.T
-
-                @pl.when(c >= CHUNKS - 2)
-                def _():
-                    part[c] += jnp.dot(hid[k * CHUNKS + c], both_w[k], preferred_element_type=jnp.float32)
-                    at = (c - CHUNKS + 2) * rows
-                    last[k, :, pl.ds(pl.multiple_of(at, rows), rows)] = hid[k * CHUNKS + c].T
-
-            product(first, second, i)
+
+                    @pl.when(c < CHUNKS - 2)
+                    def _():
+                        flipped[k, :, pl.ds(pl.multiple_of((c - 1) * rows, group_rows), group_rows)] = two.T
+
+                    @pl.when(c >= CHUNKS - 2)
+                    def _():
+                        last[k] = two.T
+
             return inner
 
         lax.fori_loop(0, 8, one, 0)
 
-        ripe(done, lambda c: far_copy(c).start())
+        ripe(done, lambda g: far_copy(g).start())
         stages(done)
         return carry
 
     lax.fori_loop(0, CHUNKS + last_lag, step, 0)
 
-    def after(done, carry):
-        stages(done)
-        first, second = product_due(done)
-
-        @pl.when(jnp.logical_or(first, second))
-        def _():
-            def one(k, inner):
-                product(first, second, k)
-                return inner
-
-            lax.fori_loop(0, half_n, one, 0)
-
+    def owed(g, carry):
+        finish(g)
         return carry
 
-    lax.fori_loop(CHUNKS, CHUNKS + finish_lag - 1, after, 0)
+    lax.fori_loop(jnp.where(is_source, 0, FINISHED), GROUPS - 2, owed, 0)
+    first_product()
+    finish(GROUPS - 2)
+    second_product()
 
     corners = [links_used(i // 4, i // 2 % 2, i % 2) for i in range(4 * DEPTH)]
     corner = zz * 4 + y * 2 + x
@@ -446,7 +435,7 @@
         bulk(stats.at[:, pl.ds(1, n - 1)], stat_sent.at[s]).wait_send()
         bulk(stats, stat_sent.at[1 - s]).wait_send()
 
-    finish(CHUNKS - 1)
+    finish(GROUPS - 1)
 
 
 def product_kernel(total, last, term, loss_in, out, loss_out, rounded, sem):
@@ -499,7 +488,7 @@
             pltpu.VMEM((half_n, shard, 2 * width), weight.dtype),
             pltpu.VMEM((CHUNKS, rows, 2 * width), jnp.float32),
             pltpu.VMEM((CHUNKS, rows, 2 * width), jnp.float32),
-            pltpu.VMEM((CHUNKS, n, 4, rows), jnp.float32),
+            pltpu.VMEM((GROUPS, n, 4, 2 * rows), jnp.float32),
             pltpu.VMEM((1, tokens_own), jnp.int32),
             pltpu.VMEM((1, tokens_own), jnp.int32),
             pltpu.VMEM((CHUNKS, rows, LANES), jnp.int32),
@@ -509,9 +498,9 @@
             dma((1,)),
             dma((4,)),
             dma((1,)),
-            dma((CHUNKS,)),
+            dma((GROUPS,)),
             dma((2,)),
-            dma((CHUNKS,)),
+            dma((GROUPS,)),
             dma((2,)),
         ],
         compiler_params=pltpu.CompilerParams(

time: 83.1 us -> 79.9 us (0.961)
  Pallas kernels: 82.3 us -> 79.1 us
    pallas_call x1, Pallas kernels: 79.3 us -> 76.1 us  [relayed(): pl.pallas_call(functools.partial(gather_kernel, n), name='gather_logits',...]
where the time goes in v3:
time: 79.9 us; the launch traced here: 79.7 us
  Pallas kernels  79.1 us (99%)
    pallas_call x1, Pallas kernels, relayed(): pl.pallas_call(functools.partial(gather_kernel, n), name='gather_logits',...  76.1 us
    pallas_call x1, Pallas kernels, relayed(): pl.pallas_call(product_kernel, name='product', out_shape=(jax.ShapeDtypeS...  3.02 us

profile of v3, /device:TPU:0, one launch (start us, length us, event | category | flops | bytes accessed | tf_op | source)
XLA Modules:
  0.0 79.7 jit_solution(2172795916704202920)
XLA Ops:
  0.6 76.1 %gather_logits.1 = (f32[8,512,512]{2,1,0:T(8,128)S(1)}, bf16[8,512,256]{2,1,0:T(8,128)(2,1)S(1)}, bf16[8,128,512]{2,1,0:T(8,128)(2,1)S(1)}, f32[4,1,128]{2,1,0:T(1,128)S(1)}) custom-call(bf16[8,64,512]{2,1,0:T(8,128)(2,1)} %bitcast.7, bf16[8,512,512]{2,1,0:T(8,128)(2,1)} %bitcast.5, bf16[8,512,512]{2,1,0:T(8,128)(2,1)} %bitcast.6, s32[1,512]{1,0:T(1,128)} %bitcast.8), custom_call_target="tpu_custom_call" | custom-call | tf_op jit(solution)/shard_map/gather_logits/pallas_call | solution.py:473
  76.7 3.0 %product.1 = (bf16[8,512,512]{2,1,0:T(8,128)(2,1)}, f32[512]{0:T(512)}) custom-call(f32[8,512,512]{2,1,0:T(8,128)S(1)} %get-tuple-element.8.total, bf16[8,512,256]{2,1,0:T(8,128)(2,1)S(1)} %get-tuple-element.9.last, bf16[8,128,512]{2,1,0:T(8,128)(2,1)S(1)} %get-tuple-element.10.term, f32[4,1,128]{2,1,0:T(1,128)S(1)} %get-tuple-element.11.loss_in), custom_call_target="tpu_custom_call" | custom-call | tf_op jit(solution)/shard_map/product/pallas_call | solution.py:515

commit v4 on v3

--- a/solution.py
+++ b/solution.py
@@ -11,16 +11,16 @@
 PLANE, DEPTH = 4, 4
 CHUNKS = 8
 GROUPS = CHUNKS // 2
-LEAD = 4
-LAGS = ((0, 0, 1, 4, 0, 3, 4, 5), (0, 0, 1, 3, 1, 3, 4, 5), (0, 0, 2, 2, 2, 3, 5, 5), (0, 0, 2, 3, 3, 3, 5, 5))
-ORDERS = ((5, 0, 6, 3, 4, 1, 7, 2), (0, 3, 2, 5, 4, 6, 1, 7), (6, 5, 0, 1, 4, 7, 2, 3), (4, 5, 3, 0, 2, 6, 7, 1))
-TALL = (156, 62, 1, 4, 8, 40, 67, 72)
-DEEP = (4, 0, 0, 1, 0, 0, 0, 0)
-VIA = (133, 200, 63, 62, 116, 28, 123, 1)
+LEAD = 3
+LAGS = ((0, 0, 1, 3, 0, 3, 4, 5), (0, 0, 2, 2, 2, 3, 4, 5), (0, 0, 2, 3, 2, 3, 4, 5), (0, 0, 2, 2, 2, 2, 5, 5))
+ORDERS = ((6, 4, 1, 2, 5, 7, 3, 0), (4, 1, 5, 6, 7, 2, 3, 0), (3, 5, 7, 0, 1, 4, 2, 6), (2, 0, 1, 4, 3, 6, 5, 7))
+TALL = (205, 24, 2, 2, 3, 82, 5, 41)
+DEEP = (1, 0, 0, 0, 2, 0, 0, 0)
+VIA = (37, 238, 1, 253, 14, 92, 25, 192)
 FINISH_LAG = 4
 FINISHED = (CHUNKS - FINISH_LAG) // 2
 LANES = 128
-UNROLL = 4
+UNROLL = 8
 
 
 def links_used(zz, y, x):
@@ -300,7 +300,7 @@
             stat_copy(g, 1, n - d).start()
             return carry
 
-        lax.fori_loop(1, n, start, 0)
+        lax.fori_loop(1, n, start, 0, unroll=5)
 
     def finish(g):
         @pl.when(is_source)
@@ -450,7 +450,7 @@
         copy(k).start()
         return carry
 
-    lax.fori_loop(0, half_n, one, 0, unroll=4)
+    lax.fori_loop(0, half_n, one, 0, unroll=8)
     for g in range(GROUPS):
         loss_out[g * LANES : (g + 1) * LANES] = loss_in[g, 0]
 

time: 79.9 us -> 79.4 us (level)
  no operation moved by 1% of the time
where the time goes in v4:
time: 79.4 us; the launch traced here: 79.2 us
  Pallas kernels  78.6 us (99%)
    pallas_call x1, Pallas kernels, relayed(): pl.pallas_call(functools.partial(gather_kernel, n), name='gather_logits',...  75.7 us
    pallas_call x1, Pallas kernels, relayed(): pl.pallas_call(product_kernel, name='product', out_shape=(jax.ShapeDtypeS...  2.95 us

profile of v4, /device:TPU:0, one launch (start us, length us, event | category | flops | bytes accessed | tf_op | source)
XLA Modules:
  0.0 79.2 jit_solution(5644762533190171306)
XLA Ops:
  0.6 75.7 %gather_logits.1 = (f32[8,512,512]{2,1,0:T(8,128)S(1)}, bf16[8,512,256]{2,1,0:T(8,128)(2,1)S(1)}, bf16[8,128,512]{2,1,0:T(8,128)(2,1)S(1)}, f32[4,1,128]{2,1,0:T(1,128)S(1)}) custom-call(bf16[8,64,512]{2,1,0:T(8,128)(2,1)} %bitcast.7, bf16[8,512,512]{2,1,0:T(8,128)(2,1)} %bitcast.5, bf16[8,512,512]{2,1,0:T(8,128)(2,1)} %bitcast.6, s32[1,512]{1,0:T(1,128)} %bitcast.8), custom_call_target="tpu_custom_call" | custom-call | tf_op jit(solution)/shard_map/gather_logits/pallas_call | solution.py:473
  76.3 2.9 %product.1 = (bf16[8,512,512]{2,1,0:T(8,128)(2,1)}, f32[512]{0:T(512)}) custom-call(f32[8,512,512]{2,1,0:T(8,128)S(1)} %get-tuple-element.8.total, bf16[8,512,256]{2,1,0:T(8,128)(2,1)S(1)} %get-tuple-element.9.last, bf16[8,128,512]{2,1,0:T(8,128)(2,1)S(1)} %get-tuple-element.10.term, f32[4,1,128]{2,1,0:T(1,128)S(1)} %get-tuple-element.11.loss_in), custom_call_target="tpu_custom_call" | custom-call | tf_op jit(solution)/shard_map/product/pallas_call | solution.py:515
